TPU v7x, 32 devices: a whole 2x2x4 slice. The times are simulated.
32 devices in a mesh: ep: 4 (over y, x), grp: 8 (over z, core).
Axes of the slice: x: 2, y: 2, z: 4, core: 2. Of those that a mesh axis runs over, the one named last changes fastest.
Arguments:
- tokens: bfloat16 [4096, 4096], P(('ep', 'grp')), may hold values from -6 to 6
- expert_ids: int32 [4096, 8], P(('ep', 'grp')), may hold values from 0 to 127, all different within a row; in each aligned block of 128 rows (0 to 127, 128 to 255, ...) at most 16 rows name the same one
- combine: float32 [4096, 8], P(('ep', 'grp')), may hold values from 0.05 to 1
- w_gate: bfloat16 [4096, 1280], P(None, 'ep'), may hold values from -0.09375 to 0.09375
- w_up: bfloat16 [4096, 1280], P(None, 'ep'), may hold values from -0.09375 to 0.09375
- w_down: bfloat16 [1280, 4096], P('ep'), may hold values from -0.15625 to 0.15625
- bias: float32 [128], replicated, may hold values from -3 to 3
Outputs:
- mixed: bfloat16 [4096, 4096], P(('ep', 'grp'))
- new_bias: float32 [128], replicated
Inputs may be any that keep to these rules, and one draw needn't show every extreme that they name: `expert_ids`: each row names 8 different experts. Among the rows of one device no expert is named more than 16 times, a bound that some block reaches.
All inputs are finite; a program needn't handle non-finite values.
Results may differ from a plain program's by a relative error of at most 0.0057.
Values may be sent and summed in bfloat16 or wider, within the bound.
A program may use at most 64 MiB of HBM per device.

v0:
```python
import jax
import jax.numpy as jnp
from jax import lax
from jax.sharding import PartitionSpec as P

NEXP = 128
TOPK = 8
SPLIT = 4


def count_loads(expert_ids):
    experts = jnp.arange(NEXP, dtype=jnp.int32)
    local = jnp.sum(
        (expert_ids.reshape(-1)[:, None] == experts[None, :]).astype(jnp.float32), axis=0
    )
    within = lax.psum(local, "ep")
    return lax.psum(within, "grp")


def per_device(tokens, expert_ids, combine, w_gate, w_up, w_down, bias):
    n_ep = lax.axis_size("ep")
    n_grp = lax.axis_size("grp")
    tok_rows = tokens.shape[0]
    width = tokens.shape[1]
    capacity = tok_rows // 8
    win_experts = n_ep // SPLIT
    flat_ids = expert_ids.reshape(-1)
    window = jnp.arange(win_experts, dtype=jnp.int32)
    hit = (flat_ids[:, None] == window[None, :]).astype(jnp.int32)
    ranks = jnp.cumsum(hit, axis=0) - 1
    slot = jnp.sum(hit * ranks, axis=1)
    inside = jnp.sum(hit, axis=1)
    dest = jnp.where(inside > 0, flat_ids * capacity + slot, win_experts * capacity)
    slot_ids = jnp.arange(win_experts * capacity, dtype=jnp.int32)
    chosen = (slot_ids[:, None] == dest[None, :]).reshape(win_experts * capacity, tok_rows, TOPK)
    select = jnp.sum(chosen.astype(jnp.float32), axis=2)
    weights = jnp.sum(chosen.astype(jnp.float32) * combine[None, :, :], axis=2)
    buffer = jnp.dot(
        select.astype(jnp.bfloat16), tokens, preferred_element_type=jnp.float32
    ).astype(jnp.bfloat16)
    outgoing = jnp.repeat(buffer.reshape(win_experts, capacity, width), SPLIT, axis=0)
    block = lax.all_to_all(outgoing, "ep", split_axis=0, concat_axis=0, tiled=True)
    rows = block.reshape(-1, width)
    gate = jnp.dot(rows, w_gate, preferred_element_type=jnp.float32)
    upval = jnp.dot(rows, w_up, preferred_element_type=jnp.float32)
    hidden = (jax.nn.silu(gate) * upval).astype(jnp.bfloat16)
    part = jnp.dot(hidden, w_down, preferred_element_type=jnp.float32).astype(jnp.bfloat16)
    returned = lax.all_to_all(
        part.reshape(block.shape), "ep", split_axis=0, concat_axis=0, tiled=True
    )
    summed = jnp.sum(
        returned.astype(jnp.float32).reshape(win_experts, SPLIT, capacity, width), axis=1
    )
    summed = summed.reshape(win_experts * capacity, width)
    mixed = jnp.dot(
        weights.T, summed, precision=lax.Precision.HIGHEST, preferred_element_type=jnp.float32
    ).astype(jnp.bfloat16)
    load = count_loads(expert_ids)
    mean_load = jnp.float32(tok_rows * n_ep * n_grp * TOPK / NEXP)
    new_bias = bias - 0.05 * (load - mean_load) / jnp.sqrt(mean_load)
    return (mixed, new_bias)


def solution(mesh):
    return jax.shard_map(
        per_device,
        mesh=mesh,
        in_specs=(
            P(("ep", "grp"), None),
            P(("ep", "grp"), None),
            P(("ep", "grp"), None),
            P(None, "ep"),
            P(None, "ep"),
            P("ep", None),
            P(),
        ),
        out_specs=(P(("ep", "grp"), None), P()),
        check_vma=False,
    )
```

profile of v0, /device:TPU:0, one launch (start us, length us, event | category | flops | bytes accessed | tf_op | source)
XLA Modules:
  0.0 56.3 jit_solution(11772067957491407302)
XLA Ops:
  0.6 0.0 copy-start
  0.6 0.8 %fusion.8 = s32[128,8]{0,1:T(8,128)S(1)} fusion(s32[128,8]{0,1:T(8,128)} %param.8), kind=kLoop, calls=%fused_computation.21 | loop fusion | flops 2048 | bytes 8192 | tf_op jit(solution)/shard_map/convert_element_type | solution.py:29
  1.5 0.1 copy.30
  1.6 0.1 reshape.124
  1.7 0.3 reduce-window.6
  2.0 0.2 slice_reduce_fusion
  2.2 0.1 reshape.117
  2.2 0.2 reduce-window.9
  2.4 0.1 broadcast.76
  2.5 0.1 reshape.120
  2.6 0.1 copy.31
  2.7 0.0 copy-start.1
  2.7 0.9 %add_select_fusion = s32[128,8]{0,1:T(8,128)S(1)} fusion(s32[128,8]{0,1:T(8,128)S(1)} %copy.31, s32[128,8]{0,1:T(8,128)S(1)} %copy.32, s32[128,8]{0,1:T(8,128)} %param.8), kind=kLoop, calls=%fused_computation.18 | loop fusion | flops 9216 | bytes 16384 | tf_op jit(solution)/shard_map/jit(_where)/select_n | solution.py:33
  3.6 0.7 %convert_reduce_fusion.2 = (bf16[16,128]{1,0:T(8,128)(2,1)S(1)}, f32[16,128]{1,0:T(8,128)S(1)}) fusion(s32[128,8]{0,1:T(8,128)S(1)} %add_select_fusion, f32[128,8]{0,1:T(8,128)} %param.9), kind=kLoop, calls=%fused_computation.13 | loop fusion | flops 77824 | bytes 20480 | tf_op jit(solution)/shard_map/reduce_sum | solution.py:36
  4.3 1.5 %convolution_convert_fusion.2 = bf16[16,4096]{1,0:T(8,128)(2,1)S(1)} fusion(bf16[128,4096]{1,0:T(8,128)(2,1)} %param.7, bf16[16,128]{1,0:T(8,128)(2,1)S(1)} %get-tuple-element.2), kind=kOutput, calls=%fused_computation.2 | convolution fusion | flops 16842752 | bytes 1183744 | tf_op jit(solution)/shard_map/dot_general | solution.py:38
  5.8 13.5 %all_to_all.10 = bf16[4,16,4096]{2,1,0:T(8,128)(2,1)S(1)} all-to-all(bf16[4,16,4096]{2,1,0:T(8,128)(2,1)S(1)} %reshape.121), channel_id=1, replica_groups=mesh['ep'=4,'grp'=8] {'ep'}, dimensions={0} | all-to-all | bytes 1048576 | tf_op jit(solution)/shard_map/all_to_all | solution.py:42
  19.3 0.0 copy-done.1
  19.3 0.9 %fusion.10 = f32[64,320]{1,0:T(8,128)S(1)} fusion(bf16[64,4096]{1,0:T(8,128)(2,1)S(1)} %bitcast.16, bf16[4096,320]{0,1:T(8,128)(2,1)S(1)} %copy-done.1), kind=kOutput, calls=%fused_computation.25 | convolution fusion | flops 167772160 | bytes 3227648 | tf_op jit(solution)/shard_map/dot_general | solution.py:44
  20.2 0.0 copy-done
  20.2 0.0 copy-start.2
  20.3 0.0 copy-start.3
  20.3 4.7 %convolution_convert_fusion.1 = bf16[64,4096]{1,0:T(8,128)(2,1)} fusion(bf16[320,4096]{1,0:T(8,128)(2,1)S(1)} %copy-done, bf16[64,4096]{1,0:T(8,128)(2,1)S(1)} %bitcast.17, bf16[4096,320]{0,1:T(8,128)(2,1)} %param.11, f32[64,320]{1,0:T(8,128)S(1)} %fusion.10), kind=kOutput, calls=%fused_computation.1 | convolution fusion | flops 335929344 | bytes 6373376 | tf_op jit(solution)/shard_map/dot_general | solution.py:47
  25.0 3.5 %all-to-all-start.1 = ((bf16[4,16,4096]{2,1,0:T(8,128)(2,1)}), bf16[4,16,4096]{2,1,0:T(8,128)(2,1)S(1)}, u32[]{:S(2)}, u32[]{:S(2)}) async-start(bf16[4,16,4096]{2,1,0:T(8,128)(2,1)} %bitcast.18), calls=%async_computation.1 | async-start | bytes 1048576 | tf_op jit(solution)/shard_map/all_to_all | solution.py:48
  28.5 0.0 copy-done.2
  28.5 0.1 copy.33
  28.6 0.1 eq.58
  28.7 0.2 convert_reduce_fusion.1
  28.9 10.4 %psum.14 = f32[128]{0:T(128)S(1)} all-reduce(f32[128]{0:T(128)S(1)} %convert_reduce_fusion.1), channel_id=1, replica_groups=mesh['ep'=4,'grp'=8] {'ep'}, use_global_device_ids=true, to_apply=%region_6.7 | all-reduce | flops 128 | bytes 1024 | tf_op jit(solution)/shard_map/psum | solution.py:16
  39.3 13.6 %psum.15 = f32[128]{0:T(128)S(1)} all-reduce(f32[128]{0:T(128)S(1)} %psum.14), channel_id=1, replica_groups=mesh['ep'=4,'grp'=8] {'grp'}, use_global_device_ids=true, to_apply=%region_7.8 | all-reduce | flops 128 | bytes 1024 | tf_op jit(solution)/shard_map/psum | solution.py:17
  52.9 0.0 copy-done.3
  52.9 0.5 multiply_subtract_fusion
  53.4 0.0 all-to-all-done.1
  53.4 0.1 convert_reduce_fusion
  53.5 2.8 %convolution_convert_fusion = bf16[128,4096]{1,0:T(8,128)(2,1)} fusion(f32[16,128]{1,0:T(8,128)S(1)} %get-tuple-element.3, f32[16,4096]{1,0:T(8,128)S(1)} %convert_reduce_fusion), kind=kOutput, calls=%fused_computation | convolution fusion | flops 101187584 | bytes 1318912 | tf_op jit(solution)/shard_map/dot_general | solution.py:55
  (3 shorter events, 0.1 us)
Async XLA Ops:
  0.6 19.6 %copy-start = (bf16[320,4096]{1,0:T(8,128)(2,1)S(1)}, bf16[320,4096]{1,0:T(8,128)(2,1)}, u32[]{:S(2)}) copy-start(bf16[320,4096]{1,0:T(8,128)(2,1)} %param.12) | copy-start | bytes 7864324
  2.7 16.6 %copy-start.1 = (bf16[4096,320]{0,1:T(8,128)(2,1)S(1)}, bf16[4096,320]{0,1:T(8,128)(2,1)}, u32[]{:S(2)}) copy-start(bf16[4096,320]{0,1:T(8,128)(2,1)} %param.10) | copy-start | bytes 7864324
  20.2 8.2 %copy-start.2 = (s32[128,8]{0,1:T(8,128)S(1)}, s32[128,8]{0,1:T(8,128)}, u32[]{:S(2)}) copy-start(s32[128,8]{0,1:T(8,128)} %param.8) | copy-start | bytes 12292
  20.3 32.6 %copy-start.3 = (f32[128]{0:T(128)S(1)}, f32[128]{0:T(128)}, u32[]{:S(2)}) copy-start(f32[128]{0:T(128)} %param.13) | copy-start | bytes 1540
  25.0 28.4 %all-to-all-start.1 = ((bf16[4,16,4096]{2,1,0:T(8,128)(2,1)}), bf16[4,16,4096]{2,1,0:T(8,128)(2,1)S(1)}, u32[]{:S(2)}, u32[]{:S(2)}) async-start(bf16[4,16,4096]{2,1,0:T(8,128)(2,1)} %bitcast.18), calls=%async_computation.1 | async-start | bytes 1048576 | tf_op jit(solution)/shard_map/all_to_all | solution.py:48
where the time goes:
time: 56.6 us; the launch traced here: 56.3 us
  blocking collectives  37.5 us (66%)
  matrix products  9.9 us (17%)
  other arithmetic  3.71 us (7%)
  starting transfers between devices  3.47 us (6%)
  local copies, waits for them, and re-layouts  1 us (2%)
  between operations  0.72 us (1%)
    psum x1, blocking collectives, count_loads(): return lax.psum(within, 'grp')  13.6 us
    all_to_all x1, blocking collectives, per_device(): lax.all_to_all(outgoing, 'ep', split_axis=0, concat_axis=0, tiled=True)  13.5 us
    psum x1, blocking collectives, count_loads(): within = lax.psum(local, 'ep')  10.4 us
    dot_general x1, matrix products, per_device(): jnp.dot(hidden, w_down, preferred_element_type=jnp.float32)  4.74 us
    all_to_all x1, starting transfers between devices, per_device(): lax.all_to_all(part.reshape(block.shape), 'ep', split_axis=0, concat_axis...  3.47 us
    dot_general x1, matrix products, per_device(): jnp.dot(weights.T, summed, precision=lax.Precision.HIGHEST, preferred_ele...  2.81 us
    dot_general x1, matrix products, per_device(): jnp.dot(select.astype(jnp.bfloat16), tokens, preferred_element_type=jnp.f...  1.47 us
  transfers between devices with their start and end apart: 1, of which 0 were waited for; matrix products, arithmetic and copies ran while one was open for 2% of the time, Pallas kernels for 0%

commit v1 on v0

--- a/solution.py
+++ b/solution.py
@@ -1,3 +1,4 @@
+import functools
 import jax
 import jax.numpy as jnp
 from jax import lax
@@ -8,12 +9,23 @@
 SPLIT = 4
 
 
+def register_ladders(inner_x, axis_tag):
+    num = lax.axis_size(axis_tag)
+    odd = inner_x
+    for idx in [[(jj, jj ^ kk) for jj in range(num)] for kk in (1, 2, 4, 8, 16) if kk < num]:
+        odd = odd + lax.ppermute(odd, axis_name=axis_tag, perm=idx)
+    return odd
+
+
+define_steps_all = functools.partial(register_ladders, axis_tag="ep")
+
+
 def count_loads(expert_ids):
     experts = jnp.arange(NEXP, dtype=jnp.int32)
     local = jnp.sum(
         (expert_ids.reshape(-1)[:, None] == experts[None, :]).astype(jnp.float32), axis=0
     )
-    within = lax.psum(local, "ep")
+    within = define_steps_all(local)
     return lax.psum(within, "grp")
 
 

time: 56.6 us -> 56.3 us (level)
  blocking collectives: 37.5 us -> 27.1 us
  waiting for transfers between devices: 0.01 us -> 6.56 us
  starting transfers between devices: 3.47 us -> 6.98 us
    psum x1 -> x0, blocking collectives: 10.4 us -> none  [count_loads(): within = lax.psum(local, 'ep')]
    ppermute x0 -> x2, waiting for transfers between devices: none -> 6.56 us  [register_ladders(): odd = odd + lax.ppermute(odd, axis_name=axis_tag, perm=idx)]
    ppermute x0 -> x2, starting transfers between devices: none -> 3.51 us  [register_ladders(): odd = odd + lax.ppermute(odd, axis_name=axis_tag, perm=idx)]
  transfers between devices with their start and end apart: 1 -> 3, of which waited for: 0 -> 2; matrix products, arithmetic and copies ran while one was open for 2% -> 2% of each run, Pallas kernels for 0% -> 0%
where the time goes in v1:
time: 56.3 us; the launch traced here: 56 us
  blocking collectives  27.1 us (48%)
  matrix products  9.9 us (18%)
  starting transfers between devices  6.98 us (12%)
  waiting for transfers between devices  6.56 us (12%)
  other arithmetic  3.71 us (7%)
  local copies, waits for them, and re-layouts  1 us (2%)
  between operations  0.73 us (1%)
    psum x1, blocking collectives, count_loads(): return lax.psum(within, 'grp')  13.6 us
    all_to_all x1, blocking collectives, per_device(): lax.all_to_all(outgoing, 'ep', split_axis=0, concat_axis=0, tiled=True)  13.5 us
    ppermute x2, waiting for transfers between devices, register_ladders(): odd = odd + lax.ppermute(odd, axis_name=axis_tag, perm=idx)  6.56 us
    dot_general x1, matrix products, per_device(): jnp.dot(hidden, w_down, preferred_element_type=jnp.float32)  4.74 us
    ppermute x2, starting transfers between devices, register_ladders(): odd = odd + lax.ppermute(odd, axis_name=axis_tag, perm=idx)  3.51 us
    all_to_all x1, starting transfers between devices, per_device(): lax.all_to_all(part.reshape(block.shape), 'ep', split_axis=0, concat_axis...  3.47 us
    dot_general x1, matrix products, per_device(): jnp.dot(weights.T, summed, precision=lax.Precision.HIGHEST, preferred_ele...  2.81 us
    dot_general x1, matrix products, per_device(): jnp.dot(select.astype(jnp.bfloat16), tokens, preferred_element_type=jnp.f...  1.47 us
  transfers between devices with their start and end apart: 3, of which 2 were waited for; matrix products, arithmetic and copies ran while one was open for 2% of the time, Pallas kernels for 0%

profile of v1, /device:TPU:0, one launch (start us, length us, event | category | flops | bytes accessed | tf_op | source)
XLA Modules:
  0.0 56.0 jit_solution(4033066797920190463)
XLA Ops:
  0.6 0.0 copy-start
  0.6 0.8 %fusion.8 = s32[128,8]{0,1:T(8,128)S(1)} fusion(s32[128,8]{0,1:T(8,128)} %param.8), kind=kLoop, calls=%fused_computation.21 | loop fusion | flops 2048 | bytes 8192 | tf_op jit(solution)/shard_map/convert_element_type | solution.py:41
  1.5 0.1 copy.30
  1.6 0.1 reshape.124
  1.7 0.3 reduce-window.6
  2.0 0.2 slice_reduce_fusion
  2.2 0.1 reshape.117
  2.2 0.2 reduce-window.9
  2.4 0.1 broadcast.76
  2.5 0.1 reshape.120
  2.6 0.1 copy.31
  2.7 0.0 copy-start.1
  2.7 0.9 %add_select_fusion = s32[128,8]{0,1:T(8,128)S(1)} fusion(s32[128,8]{0,1:T(8,128)S(1)} %copy.31, s32[128,8]{0,1:T(8,128)S(1)} %copy.32, s32[128,8]{0,1:T(8,128)} %param.8), kind=kLoop, calls=%fused_computation.18 | loop fusion | flops 9216 | bytes 16384 | tf_op jit(solution)/shard_map/jit(_where)/select_n | solution.py:45
  3.6 0.7 %convert_reduce_fusion.2 = (bf16[16,128]{1,0:T(8,128)(2,1)S(1)}, f32[16,128]{1,0:T(8,128)S(1)}) fusion(s32[128,8]{0,1:T(8,128)S(1)} %add_select_fusion, f32[128,8]{0,1:T(8,128)} %param.9), kind=kLoop, calls=%fused_computation.13 | loop fusion | flops 77824 | bytes 20480 | tf_op jit(solution)/shard_map/reduce_sum | solution.py:48
  4.3 1.5 %convolution_convert_fusion.2 = bf16[16,4096]{1,0:T(8,128)(2,1)S(1)} fusion(bf16[128,4096]{1,0:T(8,128)(2,1)} %param.7, bf16[16,128]{1,0:T(8,128)(2,1)S(1)} %get-tuple-element.2), kind=kOutput, calls=%fused_computation.2 | convolution fusion | flops 16842752 | bytes 1183744 | tf_op jit(solution)/shard_map/dot_general | solution.py:50
  5.8 13.5 %all_to_all.10 = bf16[4,16,4096]{2,1,0:T(8,128)(2,1)S(1)} all-to-all(bf16[4,16,4096]{2,1,0:T(8,128)(2,1)S(1)} %reshape.121), channel_id=1, replica_groups=mesh['ep'=4,'grp'=8] {'ep'}, dimensions={0} | all-to-all | bytes 1048576 | tf_op jit(solution)/shard_map/all_to_all | solution.py:54
  19.3 0.0 copy-done.1
  19.3 0.9 %fusion.10 = f32[64,320]{1,0:T(8,128)S(1)} fusion(bf16[64,4096]{1,0:T(8,128)(2,1)S(1)} %bitcast.16, bf16[4096,320]{0,1:T(8,128)(2,1)S(1)} %copy-done.1), kind=kOutput, calls=%fused_computation.25 | convolution fusion | flops 167772160 | bytes 3227648 | tf_op jit(solution)/shard_map/dot_general | solution.py:56
  20.2 0.0 copy-done
  20.2 0.0 copy-start.2
  20.3 0.0 copy-start.3
  20.3 4.7 %convolution_convert_fusion.1 = bf16[64,4096]{1,0:T(8,128)(2,1)} fusion(bf16[320,4096]{1,0:T(8,128)(2,1)S(1)} %copy-done, bf16[64,4096]{1,0:T(8,128)(2,1)S(1)} %bitcast.17, bf16[4096,320]{0,1:T(8,128)(2,1)} %param.11, f32[64,320]{1,0:T(8,128)S(1)} %fusion.10), kind=kOutput, calls=%fused_computation.1 | convolution fusion | flops 335929344 | bytes 6373376 | tf_op jit(solution)/shard_map/dot_general | solution.py:59
  25.0 3.5 %all-to-all-start.1 = ((bf16[4,16,4096]{2,1,0:T(8,128)(2,1)}), bf16[4,16,4096]{2,1,0:T(8,128)(2,1)S(1)}, u32[]{:S(2)}, u32[]{:S(2)}) async-start(bf16[4,16,4096]{2,1,0:T(8,128)(2,1)} %bitcast.18), calls=%async_computation.1 | async-start | bytes 1048576 | tf_op jit(solution)/shard_map/all_to_all | solution.py:60
  28.5 0.0 copy-done.2
  28.5 0.1 copy.33
  28.6 0.1 eq.58
  28.7 0.2 convert_reduce_fusion.1
  28.9 2.0 %collective-permute-start = (f32[128]{0:T(128)S(1)}, f32[128]{0:T(128)S(1)}, u32[]{:S(2)}, u32[]{:S(2)}) collective-permute-start(f32[128]{0:T(128)S(1)} %convert_reduce_fusion.1), channel_id=1, source_target_pairs={{0,8},{8,0},{16,24},{24,16},{1,9},{9,1},{17,25},{25,17},{2,10},{10... | collective-permute-start | bytes 1544 | tf_op jit(solution)/shard_map/ppermute | solution.py:16
  31.0 4.5 %collective-permute-done = f32[128]{0:T(128)S(1)} collective-permute-done((f32[128]{0:T(128)S(1)}, f32[128]{0:T(128)S(1)}, u32[]{:S(2)}, u32[]{:S(2)}) %collective-permute-start) | collective-permute-done | bytes 544 | tf_op jit(solution)/shard_map/ppermute | solution.py:16
  35.4 1.5 %collective-permute-start.1 = (f32[128]{0:T(128)S(1)}, f32[128]{0:T(128)S(1)}, u32[]{:S(2)}, u32[]{:S(2)}) collective-permute-start(f32[128]{0:T(128)S(1)} %add.30), channel_id=1, source_target_pairs={{0,16},{8,24},{16,0},{24,8},{1,17},{9,25},{17,1},{25,9},{2,18},{10... | collective-permute-start | bytes 1544 | tf_op jit(solution)/shard_map/ppermute | solution.py:16
  36.9 2.1 %collective-permute-done.1 = f32[128]{0:T(128)S(1)} collective-permute-done((f32[128]{0:T(128)S(1)}, f32[128]{0:T(128)S(1)}, u32[]{:S(2)}, u32[]{:S(2)}) %collective-permute-start.1) | collective-permute-done | bytes 544 | tf_op jit(solution)/shard_map/ppermute | solution.py:16
  39.0 13.6 %psum.7 = f32[128]{0:T(128)S(1)} all-reduce(f32[128]{0:T(128)S(1)} %add.31), channel_id=1, replica_groups=mesh['ep'=4,'grp'=8] {'grp'}, use_global_device_ids=true, to_apply=%region_6.7 | all-reduce | flops 128 | bytes 1024 | tf_op jit(solution)/shard_map/psum | solution.py:29
  52.6 0.0 copy-done.3
  52.6 0.5 multiply_subtract_fusion
  53.1 0.0 all-to-all-done.1
  53.1 0.1 convert_reduce_fusion
  53.2 2.8 %convolution_convert_fusion = bf16[128,4096]{1,0:T(8,128)(2,1)} fusion(f32[16,128]{1,0:T(8,128)S(1)} %get-tuple-element.3, f32[16,4096]{1,0:T(8,128)S(1)} %convert_reduce_fusion), kind=kOutput, calls=%fused_computation | convolution fusion | flops 101187584 | bytes 1318912 | tf_op jit(solution)/shard_map/dot_general | solution.py:67
  (5 shorter events, 0.1 us)
Async XLA Ops:
  0.6 19.6 %copy-start = (bf16[320,4096]{1,0:T(8,128)(2,1)S(1)}, bf16[320,4096]{1,0:T(8,128)(2,1)}, u32[]{:S(2)}) copy-start(bf16[320,4096]{1,0:T(8,128)(2,1)} %param.12) | copy-start | bytes 7864324
  2.7 16.6 %copy-start.1 = (bf16[4096,320]{0,1:T(8,128)(2,1)S(1)}, bf16[4096,320]{0,1:T(8,128)(2,1)}, u32[]{:S(2)}) copy-start(bf16[4096,320]{0,1:T(8,128)(2,1)} %param.10) | copy-start | bytes 7864324
  20.2 8.2 %copy-start.2 = (s32[128,8]{0,1:T(8,128)S(1)}, s32[128,8]{0,1:T(8,128)}, u32[]{:S(2)}) copy-start(s32[128,8]{0,1:T(8,128)} %param.8) | copy-start | bytes 12292
  20.3 32.3 %copy-start.3 = (f32[128]{0:T(128)S(1)}, f32[128]{0:T(128)}, u32[]{:S(2)}) copy-start(f32[128]{0:T(128)} %param.13) | copy-start | bytes 1540
  25.0 28.1 %all-to-all-start.1 = ((bf16[4,16,4096]{2,1,0:T(8,128)(2,1)}), bf16[4,16,4096]{2,1,0:T(8,128)(2,1)S(1)}, u32[]{:S(2)}, u32[]{:S(2)}) async-start(bf16[4,16,4096]{2,1,0:T(8,128)(2,1)} %bitcast.18), calls=%async_computation.1 | async-start | bytes 1048576 | tf_op jit(solution)/shard_map/all_to_all | solution.py:60
  28.9 6.5 %collective-permute-start = (f32[128]{0:T(128)S(1)}, f32[128]{0:T(128)S(1)}, u32[]{:S(2)}, u32[]{:S(2)}) collective-permute-start(f32[128]{0:T(128)S(1)} %convert_reduce_fusion.1), channel_id=1, source_target_pairs={{0,8},{8,0},{16,24},{24,16},{1,9},{9,1},{17,25},{25,17},{2,10},{10... | collective-permute-start | bytes 1544 | tf_op jit(solution)/shard_map/ppermute | solution.py:16
  35.4 3.6 %collective-permute-start.1 = (f32[128]{0:T(128)S(1)}, f32[128]{0:T(128)S(1)}, u32[]{:S(2)}, u32[]{:S(2)}) collective-permute-start(f32[128]{0:T(128)S(1)} %add.30), channel_id=1, source_target_pairs={{0,16},{8,24},{16,0},{24,8},{1,17},{9,25},{17,1},{25,9},{2,18},{10... | collective-permute-start | bytes 1544 | tf_op jit(solution)/shard_map/ppermute | solution.py:16
